TPU v7x, 32 devices: a whole 2x2x4 slice. The times are simulated.
32 devices in a mesh: band: 4 (over z), sector: 8 (over y, x, core).
Axes of the slice: x: 2, y: 2, z: 4, core: 2. Of those that a mesh axis runs over, the one named last changes fastest.
Arguments:
- field: float32 [2, 640, 2, 2560], P(None, 'band', None, 'sector'), may hold values from -6 to 6
- depart: int32 [2, 640, 80], P(None, 'band', 'sector'), may hold values from -2 to 2
- interp_weight: bfloat16 [2, 640, 80, 64, 32], P(None, 'band', 'sector'), may hold values from -0.75 to 0.75
- legendre: float32 [640, 640, 1281], P('sector', 'band'), may hold values from -0.25 to 0.25
- damping: float32 [2], replicated, may hold values from 0.3 to 30
Outputs:
- new_field: float32 [2, 640, 2, 2560], P(None, 'band', None, 'sector')
All inputs are finite; a program needn't handle non-finite values.
Results may differ from a plain program's by a relative error of at most 0.0003.
Values sent between devices are 32-bit elements; how exact they have to be, the bound alone decides.
No kernel may reach another device: no remote copies, remote signals or barrier semaphores. Data moves between devices by JAX's collectives and lax.ppermute only.
A program may use at most 192 MiB of HBM per device.

v0:
```python
import math
import jax
import jax.numpy as jnp
from jax import lax
from jax.sharding import PartitionSpec as P

HIGHEST = lax.Precision.HIGHEST


def padded(x, sides, width):
    for axis, dim in sides:
        peers, length = (lax.axis_size(axis), x.shape[dim])
        up = [(i, (i + 1) % peers) for i in range(peers)]
        down = [(j, i) for i, j in up]
        last = lax.slice_in_dim(x, length - width, length, axis=dim)
        leading = lax.slice_in_dim(x, 0, width, axis=dim)
        before = lax.ppermute(last, axis, up)
        after = lax.ppermute(leading, axis, down)
        x = jnp.concatenate([before, x, after], axis=dim)
    return x


def phase(product, lon_count):
    return 2.0 * math.pi / lon_count * (product % lon_count).astype(jnp.float32)


def forward_table(lon_count, m_count, pair_total):
    longitude = jnp.arange(lon_count, dtype=jnp.int32)[:, None]
    pair_range = jnp.arange(pair_total, dtype=jnp.int32)[None, :]
    lower_angle = phase(longitude * pair_range, lon_count)
    upper_angle = phase(longitude * (m_count - 1 - pair_range), lon_count)
    table = jnp.stack(
        [jnp.cos(lower_angle), -jnp.sin(lower_angle), jnp.cos(upper_angle), -jnp.sin(upper_angle)],
        axis=1,
    )
    return table / lon_count


def inverse_table(lon_count, m_count, pair_total):
    pair_range = jnp.arange(pair_total, dtype=jnp.int32)[:, None]
    longitude = jnp.arange(lon_count, dtype=jnp.int32)[None, :]
    lower_angle = phase(pair_range * longitude, lon_count)
    upper_angle = phase((m_count - 1 - pair_range) * longitude, lon_count)
    lower_scale = jnp.where(pair_range == 0, 1.0, 2.0)
    return jnp.stack(
        [
            lower_scale * jnp.cos(lower_angle),
            -lower_scale * jnp.sin(lower_angle),
            2.0 * jnp.cos(upper_angle),
            -2.0 * jnp.sin(upper_angle),
        ],
        axis=0,
    )


def pair_masks(pair_index, m_count, row_count):
    column = jnp.arange(row_count, dtype=jnp.int32)[None, :]
    limit = (m_count - pair_index)[:, None]
    leading = column < limit
    lag_value = jnp.where(leading, column, column - limit)
    odd_rows = lag_value % 2 == 1
    degree = jnp.where(leading, pair_index[:, None] + column, column - 1)
    return (leading, odd_rows, degree)


def analyse(wave, legendre, leading, odd_rows):
    stacked = jnp.stack([wave[0] + wave[1], wave[0] - wave[1]])
    product = jnp.einsum("svcpl,plk->svcpk", stacked, legendre, precision=HIGHEST)
    chosen = jnp.where(odd_rows, product[1], product[0])
    return jnp.where(leading, chosen[:, 0:2], chosen[:, 2:4])


def solve_modes(spectrum, damping_levels, degree, m_count):
    ratio = (degree * (degree + 1)).astype(jnp.float32) / float(m_count * m_count)
    return spectrum / (1.0 + damping_levels[:, None, None, None] * ratio[None, None])


def synthesise(spectrum, legendre, leading, odd_rows):
    lower = jnp.where(leading, spectrum, 0.0)
    upper = jnp.where(leading, 0.0, spectrum)
    northern = jnp.concatenate([lower, upper], axis=1)
    southern = jnp.where(odd_rows, -northern, northern)
    stacked = jnp.stack([northern, southern])
    return jnp.einsum("hvcpk,plk->hvcpl", stacked, legendre, precision=HIGHEST)


def advect(field, depart, interp_weight):
    tile_width = interp_weight.shape[-1]
    tile_count = depart.shape[2]
    extended = padded(field, (("sector", 3),), 3 * tile_width)
    pieces = extended.reshape(
        field.shape[0], field.shape[1], field.shape[2], tile_count + 6, tile_width
    )
    window = jnp.zeros(field.shape[:3] + (tile_count, 2 * tile_width), jnp.float32)
    for offset in range(-2, 3):
        lead_part = pieces[:, :, :, 3 + offset : 3 + offset + tile_count]
        next_part = pieces[:, :, :, 4 + offset : 4 + offset + tile_count]
        candidate = jnp.concatenate([lead_part, next_part], axis=4)
        window = jnp.where((depart == offset)[:, :, None, :, None], candidate, window)
    result = jnp.einsum(
        "hlvtj,hltji->hlvti", window, interp_weight.astype(jnp.float32), precision=HIGHEST
    )
    return result.reshape(field.shape)


def local(field, depart, interp_weight, legendre, damping):
    advected = advect(field, depart, interp_weight)
    columns = lax.all_to_all(advected, "sector", split_axis=1, concat_axis=3, tiled=True)
    lon_count = columns.shape[3]
    row_count = legendre.shape[2]
    m_count = row_count - 1
    pair_total = m_count // 2
    fourier = jnp.einsum(
        "hlvn,ncp->hvcpl", columns, forward_table(lon_count, m_count, pair_total), precision=HIGHEST
    )
    wave = lax.all_to_all(fourier, "sector", split_axis=3, concat_axis=4, tiled=True)
    pair_local = legendre.shape[0]
    pair_index = lax.axis_index("sector") * pair_local + jnp.arange(pair_local, dtype=jnp.int32)
    leading, odd_rows, degree = pair_masks(pair_index, m_count, row_count)
    partial_value = analyse(wave, legendre, leading, odd_rows)
    summed = lax.psum(partial_value, "band")
    spectrum = solve_modes(summed, damping, degree, m_count)
    synthesis = synthesise(spectrum, legendre, leading, odd_rows)
    returned = lax.all_to_all(synthesis, "sector", split_axis=4, concat_axis=3, tiled=True)
    gridded = jnp.einsum(
        "hvcpl,cpn->hlvn",
        returned,
        inverse_table(lon_count, m_count, pair_total),
        precision=HIGHEST,
    )
    return lax.all_to_all(gridded, "sector", split_axis=3, concat_axis=1, tiled=True)


def solution(mesh):
    return jax.shard_map(
        local,
        mesh=mesh,
        in_specs=(
            P(None, "band", None, "sector"),
            P(None, "band", "sector"),
            P(None, "band", "sector", None, None),
            P("sector", "band", None),
            P(),
        ),
        out_specs=P(None, "band", None, "sector"),
        check_vma=False,
    )
```

profile of v0, /device:TPU:0, one launch (start us, length us, event | category | flops | bytes accessed | tf_op | source)
XLA Modules:
  0.0 574.6 jit_solution(14221418994076441532)
XLA Ops:
  8.7 2.9 collective-permute-start.1
  11.6 28.4 %fusion.32 = (f32[2560,1,640]{2,0,1:T(8,128)}, f32[2560,1,640]{2,0,1:T(8,128)}) fusion(s32[640]{0:T(1024)S(1)} %iota_subtract_fusion), kind=kLoop, calls=%fused_computation.40 | loop fusion | flops 16384000 | bytes 13109760 | tf_op jit(solution)/shard_map/cos | solution.py:33
  40.2 47.9 %copy.114 = bf16[2,160,10,64,32]{3,4,2,1,0:T(8,128)(2,1)} copy(bf16[2,160,10,64,32]{1,4,3,2,0:T(8,128)(2,1)} %param.7) | data formatting | bytes 26214400 | tf_op args[2]
  91.1 3.6 copy.113
  94.7 43.8 %convolution_bitcast_fusion = f32[2,160,2,10,32]{4,2,3,1,0:T(2,128)S(1)} fusion(f32[2,160,2,10,64]{4,2,3,1,0:T(2,128)} %copy.113, bf16[2,160,10,64,32]{3,4,2,1,0:T(8,128)(2,1)} %copy.114), kind=kOutput, calls=%fused_computation.67 | convolution fusion | flops 157286400 | bytes 15564800 | tf_op jit(solution)/shard_map/hlvtj,hltji->hlvti/dot_general | solution.py:100
  138.4 3.4 copy.115
  144.2 4.0 all-to-all-start
  148.2 27.9 %sine_negate_fusion.1 = (f32[2560,1,640]{2,0,1:T(8,128)}, f32[2560,1,640]{2,0,1:T(8,128)}) fusion(), kind=kLoop, calls=%fused_computation.41 | loop fusion | flops 16384000 | bytes 13107200 | tf_op jit(solution)/shard_map/neg | solution.py:33
  176.7 19.3 %fusion.54 = f32[2,2,4,640,20]{3,4,1,0,2:T(8,128)S(1)} fusion(f32[2,20,2,2560,1]{3,1,2,0,4:T(8,128)S(1)} %reshape.528, f32[2560,1,640]{2,0,1:T(8,128)} %get-tuple-element.25, f32[2560,1,640]{2,0,1:T(8,128)} %get-tuple-element.24, f32[2560,1,640]{2,0,1:T(8,128)} %get-tuple-element.30, f32[2560,1,640]{2,0,1:T(8,128)} %get-tuple-element.31), kind=kOutput, calls=%fused_computation.78 | convolution fusion | flops 6317670400 | bytes 27852800 | tf_op jit(solution)/shard_map/hlvn,ncp->hvcpl/dot_general | solution.py:113
  196.0 5.0 copy.120
  201.0 10.6 %reshape.535 = f32[8,1,25600]{2,1,0:T(1,128)} reshape(f32[640,4,2,2,20]{4,3,2,1,0:T(2,128)} %bitcast.90) | data formatting | bytes 1638400
  211.6 4.2 all-to-all-start.1
  217.1 11.6 %all-to-all-done.1 = f32[8,1,25600]{2,1,0:T(1,128)S(1)} async-done(((f32[8,1,25600]{2,1,0:T(1,128)}), f32[8,1,25600]{2,1,0:T(1,128)S(1)}, u32[]{:S(2)}, u32[]{:S(2)}) %all-to-all-start.1) | async-done | bytes 819232 | tf_op jit(solution)/shard_map/all_to_all | solution.py:116
  229.2 2.6 reduce
  231.8 10.9 %reshape.536 = f32[640,4,2,2,20]{4,3,2,1,0:T(2,128)} reshape(f32[8,25600]{1,0:T(8,128)S(1)} %reduce) | data formatting | bytes 1638400
  242.7 6.0 %copy.141 = f32[2,2,4,8,80,20]{4,3,2,5,1,0:T(8,128)S(1)} copy(f32[2,2,4,8,80,20]{5,1,0,2,4,3:T(2,128)} %bitcast.91) | data formatting | bytes 1638400 | tf_op jit(solution)/shard_map/all_to_all | solution.py:116
  250.4 42.7 %fusion.44 = f32[2,2,4,80,1281]{4,2,1,0,3:T(4,128)} fusion(f32[80,160,1281]{2,1,0:T(8,128)} %param.8, f32[2,2,4,80,160]{4,2,1,0,3:T(4,128)S(1)} %fusion.83), kind=kOutput, calls=%fused_computation.61 | convolution fusion | flops 3148185600 | bytes 72965120 | tf_op jit(solution)/shard_map/svcpl,plk->svcpk/dot_general | solution.py:68
  293.2 4.5 fusion.48
  297.6 2.6 slice_select_fusion
  300.8 28.3 %sine_multiply_fusion.1 = (f32[1,640,2560]{2,1,0:T(8,128)}, f32[1,640,2560]{2,1,0:T(8,128)}) fusion(f32[640]{0:T(1024)S(1)} %fusion.65, f32[640]{0:T(1024)S(1)} %fusion.64), kind=kLoop, calls=%fused_computation.51 | loop fusion | flops 18022400 | bytes 13112320 | tf_op jit(solution)/shard_map/mul | solution.py:48
  329.0 48.0 %all-reduce.2.cloned.1.call-done = f32[2,2,80,1281]{3,1,0,2:T(2,128)} async-done(((f32[2,2,80,1281]{3,1,0,2:T(2,128)}), f32[2,2,80,1281]{3,1,0,2:T(2,128)}) %all-reduce.2.cloned.1.call-update) | async-done | bytes 1639696 | tf_op jit(solution)/shard_map/psum | solution.py:121
  377.0 3.1 broadcast_select_fusion.1
  386.5 73.3 %fusion.49 = f32[2,2,4,80,160]{4,2,1,0,3:T(4,128)S(1)} fusion(f32[80,160,1281]{2,1,0:T(8,128)} %param.8, f32[1,2,4,80,1281]{4,2,1,3,0:T(4,128)S(1)} %negate_select_fusion, f32[1,2,4,80,1281]{4,2,1,3,0:T(4,128)S(1)} %maximum_bitcast_fusion.4), kind=kOutput, calls=%fused_computation.77 | convolution fusion | flops 3149825280 | bytes 72965120 | tf_op jit(solution)/shard_map/hvcpk,plk->hvcpl/dot_general | solution.py:84
  461.4 4.1 all-to-all-start.2
  465.6 29.7 %cosine_multiply_fusion = (f32[1,640,2560]{2,1,0:T(8,128)}, f32[1,640,2560]{2,1,0:T(8,128)}) fusion(s32[640]{0:T(1024)S(1)} %iota_subtract_fusion), kind=kLoop, calls=%fused_computation.47 | loop fusion | flops 18022400 | bytes 13109760 | tf_op jit(solution)/shard_map/mul | solution.py:49
  496.5 19.2 %fusion.47 = f32[2,20,2,2560]{3,1,2,0:T(8,128)S(1)} fusion(f32[2,2,4,640,20]{3,4,2,1,0:T(8,128)S(1)} %reshape.534, f32[1,640,2560]{2,1,0:T(8,128)} %get-tuple-element.23, f32[1,640,2560]{2,1,0:T(8,128)} %get-tuple-element.22, f32[1,640,2560]{2,1,0:T(8,128)} %get-tuple-element.32, f32[1,640,2560]{2,1,0:T(8,128)} %get-tuple-element.33), kind=kOutput, calls=%fused_computation.62 | convolution fusion | flops 6311116800 | bytes 27852800 | tf_op jit(solution)/shard_map/hvcpl,cpn->hlvn/dot_general | solution.py:125
  515.7 5.0 copy.132
  520.7 9.9 %reshape.537 = f32[8,1,25600]{2,1,0:T(1,128)S(1)} reshape(f32[2560,2,2,20]{3,2,1,0:T(2,128)} %bitcast.92) | data formatting | bytes 1638400
  530.6 17.1 %all_to_all.69 = f32[8,1,25600]{2,1,0:T(1,128)S(1)} all-to-all(f32[8,1,25600]{2,1,0:T(1,128)S(1)} %reshape.537), channel_id=1, replica_groups=mesh['band'=4,'sector'=8] {'sector'}, dimensions={0} | all-to-all | bytes 1638400 | tf_op jit(solution)/shard_map/all_to_all | solution.py:131
  547.7 2.6 reduce.1
  550.3 10.9 %reshape.538 = f32[2560,2,2,20]{3,2,1,0:T(2,128)} reshape(f32[8,25600]{1,0:T(8,128)S(1)} %reduce.1) | data formatting | bytes 1638400
  561.1 5.0 copy.144
  (50 shorter events, 22.8 us)
Async XLA Ops:
  8.2 79.9 %collective-permute-start = (f32[2,160,2,96]{1,3,2,0:T(8,128)S(1)}, f32[2,160,2,96]{1,3,2,0:T(8,128)S(1)}, u32[]{:S(2)}, u32[]{:S(2)}) collective-permute-start(f32[2,160,2,96]{1,3,2,0:T(8,128)S(1)} %get-tuple-element.15), channel_id=1, source_target_pairs={{0,1},{1,2},{2,3},{3,4},{4,5},{5,6},{6,7},{7,0},{8,9},{9,10},{10,1... | collective-permute-start | bytes 737288 | tf_op jit(solution)/shard_map/ppermute | solution.py:17
  8.7 79.4 %collective-permute-start.1 = (f32[2,160,2,96]{1,3,2,0:T(8,128)S(1)}, f32[2,160,2,96]{1,3,2,0:T(8,128)S(1)}, u32[]{:S(2)}, u32[]{:S(2)}) collective-permute-start(f32[2,160,2,96]{1,3,2,0:T(8,128)S(1)} %get-tuple-element.16), channel_id=1, source_target_pairs={{1,0},{2,1},{3,2},{4,3},{5,4},{6,5},{7,6},{0,7},{9,8},{10,9},{11,1... | collective-permute-start | bytes 737288 | tf_op jit(solution)/shard_map/ppermute | solution.py:18
  11.6 28.4 %copy-start.1 = (s32[2,160,10]{1,0,2:T(2,128)S(1)}, s32[2,160,10]{1,0,2:T(2,128)}, u32[]{:S(2)}) copy-start(s32[2,160,10]{1,0,2:T(2,128)} %param.6) | copy-start | bytes 38404
  144.2 31.9 %all-to-all-start = ((f32[2,160,2,320]{3,2,0,1:T(2,128)}), f32[2,160,2,320]{3,2,0,1:T(2,128)S(1)}, u32[]{:S(2)}, u32[]{:S(2)}) async-start(f32[2,160,2,320]{3,2,0,1:T(2,128)} %copy.116), calls=%async_computation | async-start | bytes 1966080 | tf_op jit(solution)/shard_map/all_to_all | solution.py:108
  211.6 17.1 %all-to-all-start.1 = ((f32[8,1,25600]{2,1,0:T(1,128)}), f32[8,1,25600]{2,1,0:T(1,128)S(1)}, u32[]{:S(2)}, u32[]{:S(2)}) async-start(f32[8,1,25600]{2,1,0:T(1,128)} %reshape.535), calls=%async_computation.1 | async-start | bytes 1638400 | tf_op jit(solution)/shard_map/all_to_all | solution.py:116
  215.8 161.2 %all-reduce.2.cloned.1.call-start = ((), (), s32[]{:S(2)}) async-start(), calls=%async_computation.4 | async-start | bytes 3604480 | tf_op jit(solution)/shard_map/psum | solution.py:121
  250.4 42.8 %copy-start = (pred[80,1281]{1,0:T(8,128)(4,1)S(1)}, pred[80,1281]{1,0:T(8,128)(4,1)}, u32[]{:S(2)}) copy-start(pred[80,1281]{1,0:T(8,128)(4,1)} %get-tuple-element.26) | copy-start | bytes 307444
  297.6 2.7 copy-start.2
  461.4 33.8 %all-to-all-start.2 = ((f32[2,2,4,80,160]{3,2,1,0,4:T(4,128)}), f32[2,2,4,80,160]{3,2,1,0,4:T(4,128)S(1)}, u32[]{:S(2)}, u32[]{:S(2)}) async-start(f32[2,2,4,80,160]{3,2,1,0,4:T(4,128)} %copy.128), calls=%async_computation.2 | async-start | bytes 2621440 | tf_op jit(solution)/shard_map/all_to_all | solution.py:124
Sparse Core Ops, SparseCore 0:
  300.4 76.5 all-reduce.1
where the time goes:
time: 584 us; the launch traced here: 575 us
  matrix products  198 us (34%)
  other arithmetic  140 us (24%)
  local copies, waits for them, and re-layouts  130 us (22%)
  waiting for transfers between devices  59.6 us (10%)
  blocking collectives  17.1 us (3%)
  starting transfers between devices  15.9 us (3%)
  between operations  13.9 us (2%)
    unnamed x12, local copies, waits for them, and re-layouts  91.7 us
    dot_general x1, matrix products, synthesise(): return jnp.einsum('hvcpk,plk->hvcpl', stacked, legendre, precision=HIGHEST)  73.3 us
    psum x1, waiting for transfers between devices, local(): summed = lax.psum(partial_value, 'band')  48 us
    dot_general x1, matrix products, advect(): jnp.einsum('hlvtj,hltji->hlvti', window, interp_weight.astype(jnp.float32...  43.8 us
    dot_general x1, matrix products, analyse(): jnp.einsum('svcpl,plk->svcpk', stacked, legendre, precision=HIGHEST)  42.7 us
    mul x1, other arithmetic, inverse_table(): 2.0 * jnp.cos(upper_angle)  29.7 us
    cos x1, other arithmetic, forward_table(): jnp.cos(upper_angle)  28.4 us
    mul x1, other arithmetic, inverse_table(): -lower_scale * jnp.sin(lower_angle)  28.3 us
  transfers between devices with their start and end apart: 6, of which 2 were waited for; matrix products, arithmetic and copies ran while one was open for 29% of the time, Pallas kernels for 0%

commit v1 on v0

--- a/solution.py
+++ b/solution.py
@@ -3,6 +3,7 @@
 import jax.numpy as jnp
 from jax import lax
 from jax.sharding import PartitionSpec as P
+from jax.lax import axis_size, ppermute
 
 HIGHEST = lax.Precision.HIGHEST
 
@@ -118,7 +119,12 @@
     pair_index = lax.axis_index("sector") * pair_local + jnp.arange(pair_local, dtype=jnp.int32)
     leading, odd_rows, degree = pair_masks(pair_index, m_count, row_count)
     partial_value = analyse(wave, legendre, leading, odd_rows)
-    summed = lax.psum(partial_value, "band")
+    summed = partial_value
+    chips = axis_size("band")
+    for at in [t for t in (1, 2, 4, 8, 16) if t < chips]:
+        summed = summed + ppermute(
+            summed, axis_name="band", perm=[(b, b ^ at) for b in range(chips)]
+        )
     spectrum = solve_modes(summed, damping, degree, m_count)
     synthesis = synthesise(spectrum, legendre, leading, odd_rows)
     returned = lax.all_to_all(synthesis, "sector", split_axis=4, concat_axis=3, tiled=True)

time: 584 us -> 614 us (1.051)
  waiting for transfers between devices: 59.6 us -> 94.6 us
  between operations: 13.9 us -> 0.55 us
  starting transfers between devices: 15.9 us -> 25.2 us
    ppermute x0 -> x2, waiting for transfers between devices: none -> 82.1 us  [local(): ppermute(summed, axis_name='band', perm=[(b, b ^ at) for b in range(chips)])]
    psum x1 -> x0, waiting for transfers between devices: 48 us -> none  [local(): summed = lax.psum(partial_value, 'band')]
    unnamed x12 -> x10, local copies, waits for them, and re-layouts: 91.7 us -> 91.8 us
  transfers between devices with their start and end apart: 6 -> 7, of which waited for: 2 -> 3; matrix products, arithmetic and copies ran while one was open for 29% -> 27% of each run, Pallas kernels for 0% -> 0%
where the time goes in v1:
time: 614 us; the launch traced here: 604 us
  matrix products  198 us (32%)
  other arithmetic  139 us (23%)
  local copies, waits for them, and re-layouts  130 us (21%)
  waiting for transfers between devices  94.6 us (15%)
  starting transfers between devices  25.2 us (4%)
  blocking collectives  17.1 us (3%)
    unnamed x10, local copies, waits for them, and re-layouts  91.8 us
    ppermute x2, waiting for transfers between devices, local(): ppermute(summed, axis_name='band', perm=[(b, b ^ at) for b in range(chips)])  82.1 us
    dot_general x1, matrix products, synthesise(): return jnp.einsum('hvcpk,plk->hvcpl', stacked, legendre, precision=HIGHEST)  73 us
    dot_general x1, matrix products, advect(): jnp.einsum('hlvtj,hltji->hlvti', window, interp_weight.astype(jnp.float32...  43.8 us
    dot_general x1, matrix products, analyse(): jnp.einsum('svcpl,plk->svcpk', stacked, legendre, precision=HIGHEST)  42.9 us
    mul x1, other arithmetic, inverse_table(): 2.0 * jnp.cos(upper_angle)  29.7 us
    cos x1, other arithmetic, forward_table(): jnp.cos(upper_angle)  28.3 us
    mul x1, other arithmetic, inverse_table(): -lower_scale * jnp.sin(lower_angle)  28.3 us
  transfers between devices with their start and end apart: 7, of which 3 were waited for; matrix products, arithmetic and copies ran while one was open for 27% of the time, Pallas kernels for 0%

profile of v1, /device:TPU:0, one launch (start us, length us, event | category | flops | bytes accessed | tf_op | source)
XLA Modules:
  0.0 604.3 jit_solution(10196253147172846542)
XLA Ops:
  2.2 2.9 collective-permute-start.1
  5.1 28.3 %fusion.32 = (f32[2560,1,640]{2,0,1:T(8,128)}, f32[2560,1,640]{2,0,1:T(8,128)}) fusion(s32[640]{0:T(1024)S(1)} %iota_subtract_fusion), kind=kLoop, calls=%fused_computation.40 | loop fusion | flops 16384000 | bytes 13109760 | tf_op jit(solution)/shard_map/cos | solution.py:34
  33.6 47.9 %copy.114 = bf16[2,160,10,64,32]{3,4,2,1,0:T(8,128)(2,1)} copy(bf16[2,160,10,64,32]{1,4,3,2,0:T(8,128)(2,1)} %param.7) | data formatting | bytes 26214400 | tf_op args[2]
  84.5 3.6 copy.113
  88.1 43.8 %convolution_bitcast_fusion = f32[2,160,2,10,32]{4,2,3,1,0:T(2,128)S(1)} fusion(f32[2,160,2,10,64]{4,2,3,1,0:T(2,128)} %copy.113, bf16[2,160,10,64,32]{3,4,2,1,0:T(8,128)(2,1)} %copy.114), kind=kOutput, calls=%fused_computation.67 | convolution fusion | flops 157286400 | bytes 15564800 | tf_op jit(solution)/shard_map/hlvtj,hltji->hlvti/dot_general | solution.py:101
  131.9 3.4 copy.115
  137.6 3.8 all-to-all-start
  141.5 27.9 %sine_negate_fusion.1 = (f32[2560,1,640]{2,0,1:T(8,128)}, f32[2560,1,640]{2,0,1:T(8,128)}) fusion(), kind=kLoop, calls=%fused_computation.41 | loop fusion | flops 16384000 | bytes 13107200 | tf_op jit(solution)/shard_map/neg | solution.py:34
  170.0 19.3 %fusion.54 = f32[2,2,4,640,20]{3,4,1,0,2:T(8,128)S(1)} fusion(f32[2,20,2,2560,1]{3,1,2,0,4:T(8,128)S(1)} %reshape.528, f32[2560,1,640]{2,0,1:T(8,128)} %get-tuple-element.25, f32[2560,1,640]{2,0,1:T(8,128)} %get-tuple-element.24, f32[2560,1,640]{2,0,1:T(8,128)} %get-tuple-element.30, f32[2560,1,640]{2,0,1:T(8,128)} %get-tuple-element.31), kind=kOutput, calls=%fused_computation.79 | convolution fusion | flops 6317670400 | bytes 27852800 | tf_op jit(solution)/shard_map/hlvn,ncp->hvcpl/dot_general | solution.py:114
  189.3 5.0 copy.120
  194.3 10.6 %reshape.535 = f32[8,1,25600]{2,1,0:T(1,128)} reshape(f32[640,4,2,2,20]{4,3,2,1,0:T(2,128)} %bitcast.90) | data formatting | bytes 1638400
  204.9 4.7 all-to-all-start.1
  210.0 12.5 %all-to-all-done.1 = f32[8,1,25600]{2,1,0:T(1,128)S(1)} async-done(((f32[8,1,25600]{2,1,0:T(1,128)}), f32[8,1,25600]{2,1,0:T(1,128)S(1)}, u32[]{:S(2)}, u32[]{:S(2)}) %all-to-all-start.1) | async-done | bytes 819232 | tf_op jit(solution)/shard_map/all_to_all | solution.py:117
  223.0 2.6 reduce
  225.6 10.9 %reshape.536 = f32[640,4,2,2,20]{4,3,2,1,0:T(2,128)} reshape(f32[8,25600]{1,0:T(8,128)S(1)} %reduce) | data formatting | bytes 1638400
  236.5 5.8 copy.141
  244.1 42.9 %fusion.44 = f32[2,2,4,80,1281]{4,2,1,0,3:T(4,128)} fusion(f32[80,160,1281]{2,1,0:T(8,128)} %param.8, f32[2,2,4,80,160]{4,2,1,0,3:T(4,128)S(1)} %fusion.84), kind=kOutput, calls=%fused_computation.61 | convolution fusion | flops 3148185600 | bytes 72965120 | tf_op jit(solution)/shard_map/svcpl,plk->svcpk/dot_general | solution.py:69
  286.9 4.5 fusion.48
  295.4 36.3 %collective-permute-done.2 = f32[2,2,80,1281]{3,1,0,2:T(2,128)S(1)} collective-permute-done((f32[2,2,80,1281]{3,1,0,2:T(2,128)S(1)}, f32[2,2,80,1281]{3,1,0,2:T(2,128)S(1)}, u32[]{:S(2)}, u32[]{:S(2)}) %collective-permute-start.2) | collective-permute-done | bytes 1639712 | tf_op jit(solution)/shard_map/ppermute | solution.py:125
  333.4 2.8 collective-permute-start.3
  336.7 28.3 %sine_multiply_fusion.1 = (f32[1,640,2560]{2,1,0:T(8,128)}, f32[1,640,2560]{2,1,0:T(8,128)}) fusion(f32[640]{0:T(1024)S(1)} %fusion.65, f32[640]{0:T(1024)S(1)} %fusion.64), kind=kLoop, calls=%fused_computation.51 | loop fusion | flops 18022400 | bytes 13112320 | tf_op jit(solution)/shard_map/mul | solution.py:49
  365.0 45.8 %collective-permute-done.3 = f32[2,2,80,1281]{3,1,0,2:T(2,128)S(1)} collective-permute-done((f32[2,2,80,1281]{3,1,0,2:T(2,128)S(1)}, f32[2,2,80,1281]{3,1,0,2:T(2,128)S(1)}, u32[]{:S(2)}, u32[]{:S(2)}) %collective-permute-start.3) | collective-permute-done | bytes 1639712 | tf_op jit(solution)/shard_map/ppermute | solution.py:125
  419.4 73.0 %fusion.49 = f32[2,2,4,80,160]{4,2,1,0,3:T(4,128)S(1)} fusion(f32[80,160,1281]{2,1,0:T(8,128)} %param.8, f32[1,2,4,80,1281]{4,2,1,3,0:T(4,128)S(1)} %negate_select_fusion, f32[1,2,4,80,1281]{4,2,1,3,0:T(4,128)S(1)} %maximum_bitcast_fusion.4), kind=kOutput, calls=%fused_computation.78 | convolution fusion | flops 3149825280 | bytes 72965120 | tf_op jit(solution)/shard_map/hvcpk,plk->hvcpl/dot_general | solution.py:85
  494.1 8.0 %all-to-all-start.2 = ((f32[2,2,4,80,160]{3,2,1,0,4:T(4,128)}), f32[2,2,4,80,160]{3,2,1,0,4:T(4,128)S(1)}, u32[]{:S(2)}, u32[]{:S(2)}) async-start(f32[2,2,4,80,160]{3,2,1,0,4:T(4,128)} %copy.128), calls=%async_computation.2 | async-start | bytes 2621440 | tf_op jit(solution)/shard_map/all_to_all | solution.py:130
  502.1 29.7 %cosine_multiply_fusion = (f32[1,640,2560]{2,1,0:T(8,128)}, f32[1,640,2560]{2,1,0:T(8,128)}) fusion(s32[640]{0:T(1024)S(1)} %iota_subtract_fusion), kind=kLoop, calls=%fused_computation.47 | loop fusion | flops 18022400 | bytes 13109760 | tf_op jit(solution)/shard_map/mul | solution.py:50
  533.0 19.2 %fusion.47 = f32[2,20,2,2560]{3,1,2,0:T(8,128)S(1)} fusion(f32[2,2,4,640,20]{3,4,2,1,0:T(8,128)S(1)} %reshape.534, f32[1,640,2560]{2,1,0:T(8,128)} %get-tuple-element.23, f32[1,640,2560]{2,1,0:T(8,128)} %get-tuple-element.22, f32[1,640,2560]{2,1,0:T(8,128)} %get-tuple-element.32, f32[1,640,2560]{2,1,0:T(8,128)} %get-tuple-element.33), kind=kOutput, calls=%fused_computation.62 | convolution fusion | flops 6311116800 | bytes 27852800 | tf_op jit(solution)/shard_map/hvcpl,cpn->hlvn/dot_general | solution.py:131
  552.3 4.9 copy.132
  557.2 9.9 %reshape.537 = f32[8,1,25600]{2,1,0:T(1,128)S(1)} reshape(f32[2560,2,2,20]{3,2,1,0:T(2,128)} %bitcast.92) | data formatting | bytes 1638400
  567.1 17.1 %all_to_all.69 = f32[8,1,25600]{2,1,0:T(1,128)S(1)} all-to-all(f32[8,1,25600]{2,1,0:T(1,128)S(1)} %reshape.537), channel_id=1, replica_groups=mesh['band'=4,'sector'=8] {'sector'}, dimensions={0} | all-to-all | bytes 1638400 | tf_op jit(solution)/shard_map/all_to_all | solution.py:137
  584.2 2.6 reduce.1
  586.8 10.9 %reshape.538 = f32[2560,2,2,20]{3,2,1,0:T(2,128)} reshape(f32[8,25600]{1,0:T(8,128)S(1)} %reduce.1) | data formatting | bytes 1638400
  597.7 5.0 copy.144
  (50 shorter events, 29.9 us)
Async XLA Ops:
  1.6 79.9 %collective-permute-start = (f32[2,160,2,96]{1,3,2,0:T(8,128)S(1)}, f32[2,160,2,96]{1,3,2,0:T(8,128)S(1)}, u32[]{:S(2)}, u32[]{:S(2)}) collective-permute-start(f32[2,160,2,96]{1,3,2,0:T(8,128)S(1)} %get-tuple-element.15), channel_id=1, source_target_pairs={{0,1},{1,2},{2,3},{3,4},{4,5},{5,6},{6,7},{7,0},{8,9},{9,10},{10,1... | collective-permute-start | bytes 737288 | tf_op jit(solution)/shard_map/ppermute | solution.py:18
  2.2 79.4 %collective-permute-start.1 = (f32[2,160,2,96]{1,3,2,0:T(8,128)S(1)}, f32[2,160,2,96]{1,3,2,0:T(8,128)S(1)}, u32[]{:S(2)}, u32[]{:S(2)}) collective-permute-start(f32[2,160,2,96]{1,3,2,0:T(8,128)S(1)} %get-tuple-element.16), channel_id=1, source_target_pairs={{1,0},{2,1},{3,2},{4,3},{5,4},{6,5},{7,6},{0,7},{9,8},{10,9},{11,1... | collective-permute-start | bytes 737288 | tf_op jit(solution)/shard_map/ppermute | solution.py:19
  5.1 28.4 %copy-start = (s32[2,160,10]{1,0,2:T(2,128)S(1)}, s32[2,160,10]{1,0,2:T(2,128)}, u32[]{:S(2)}) copy-start(s32[2,160,10]{1,0,2:T(2,128)} %param.6) | copy-start | bytes 38404
  137.6 31.8 %all-to-all-start = ((f32[2,160,2,320]{3,2,0,1:T(2,128)}), f32[2,160,2,320]{3,2,0,1:T(2,128)S(1)}, u32[]{:S(2)}, u32[]{:S(2)}) async-start(f32[2,160,2,320]{3,2,0,1:T(2,128)} %copy.116), calls=%async_computation | async-start | bytes 1966080 | tf_op jit(solution)/shard_map/all_to_all | solution.py:109
  204.9 17.6 %all-to-all-start.1 = ((f32[8,1,25600]{2,1,0:T(1,128)}), f32[8,1,25600]{2,1,0:T(1,128)S(1)}, u32[]{:S(2)}, u32[]{:S(2)}) async-start(f32[8,1,25600]{2,1,0:T(1,128)} %reshape.535), calls=%async_computation.1 | async-start | bytes 1638400 | tf_op jit(solution)/shard_map/all_to_all | solution.py:117
  292.8 38.9 %collective-permute-start.2 = (f32[2,2,80,1281]{3,1,0,2:T(2,128)S(1)}, f32[2,2,80,1281]{3,1,0,2:T(2,128)S(1)}, u32[]{:S(2)}, u32[]{:S(2)}) collective-permute-start(f32[2,2,80,1281]{3,1,0,2:T(2,128)S(1)} %slice_select_fusion), channel_id=1, source_target_pairs={{0,8},{8,0},{16,24},{24,16},{1,9},{9,1},{17,25},{25,17},{2,10},{10... | collective-permute-start | bytes 4919048 | tf_op jit(solution)/shard_map/ppermute | solution.py:125
  295.4 40.9 %copy-start.1 = (f32[2]{0:T(128)S(1)}, f32[2]{0:T(128)}, u32[]{:S(2)}) copy-start(f32[2]{0:T(128)} %param.9) | copy-start | bytes 28
  333.4 77.3 %collective-permute-start.3 = (f32[2,2,80,1281]{3,1,0,2:T(2,128)S(1)}, f32[2,2,80,1281]{3,1,0,2:T(2,128)S(1)}, u32[]{:S(2)}, u32[]{:S(2)}) collective-permute-start(f32[2,2,80,1281]{3,1,0,2:T(2,128)S(1)} %fusion.77), channel_id=1, source_target_pairs={{0,16},{8,24},{16,0},{24,8},{1,17},{9,25},{17,1},{25,9},{2,18},{10... | collective-permute-start | bytes 4919048 | tf_op jit(solution)/shard_map/ppermute | solution.py:125
  494.1 37.7 %all-to-all-start.2 = ((f32[2,2,4,80,160]{3,2,1,0,4:T(4,128)}), f32[2,2,4,80,160]{3,2,1,0,4:T(4,128)S(1)}, u32[]{:S(2)}, u32[]{:S(2)}) async-start(f32[2,2,4,80,160]{3,2,1,0,4:T(4,128)} %copy.128), calls=%async_computation.2 | async-start | bytes 2621440 | tf_op jit(solution)/shard_map/all_to_all | solution.py:130
